TPU v7x, 32 devices: a whole 2x2x4 slice. The times are simulated.
32 devices in a mesh: parts: 2 (over x), seq: 16 (over z, y, core).
Axes of the slice: x: 2, y: 2, z: 4, core: 2. Of those that a mesh axis runs over, the one named last changes fastest.
Arguments:
- token_ids: int32 [4, 4], P(None, 'parts'), parts along dimension 1, may hold values from 0 to 76031
- lengths: int32 [4], P('parts'), parts along dimension 0, may hold values from 24576 to 32768, as said below
- embed_table: bfloat16 [76032, 5120], P('seq'), may hold values from -6 to 6
- attn_gain: bfloat16 [5120], replicated, may hold values from 0.25 to 1.75
- w_qkv: bfloat16 [5120, 7168], P('seq'), may hold values from -0.125 to 0.125
- qkv_bias: float32 [7168], replicated, may hold values from -8 to 8
- cache_keys: bfloat16 [4, 32768, 1024], P('parts', 'seq'), parts along dimension 0, may hold values from -300 to 300
- cache_values: bfloat16 [4, 32768, 1024], P('parts', 'seq'), parts along dimension 0, may hold values from -6 to 6
- w_out: bfloat16 [5120, 5120], P(None, 'seq'), may hold values from -0.078125 to 0.078125
- mlp_gain: bfloat16 [5120], replicated, may hold values from 0.25 to 1.75
- w_gate: bfloat16 [5120, 16384], P(None, 'seq'), may hold values from -0.078125 to 0.078125
- w_up: bfloat16 [5120, 16384], P(None, 'seq'), may hold values from -0.078125 to 0.078125
- w_down: bfloat16 [16384, 5120], P('seq'), may hold values from -0.0625 to 0.0625
Outputs:
- attended: bfloat16 [4, 4, 5120], P(None, 'parts'), parts along dimension 1
- layer_out: bfloat16 [4, 4, 5120], P(None, 'parts', 'seq'), parts along dimension 1
There are 2 independent parts, one for each index of `parts`. A program takes and returns all parts, laid end to end along the dimension named above; an argument that names none is the same for every part. Nothing has to cross between parts.
Inputs may be any that keep to these rules, and one draw needn't show every extreme that they name: Cache positions lengths[b] and later are unused; the first prompt fills the whole cache of 32768 positions.
All inputs are finite; a program needn't handle non-finite values.
Results may differ from a plain program's by a relative error of at most 0.017.
The roundings to bfloat16 on the way count: a program that leaves them out, or rounds other values in their place, can miss the bound.
Values may be sent and summed in bfloat16 or wider, within the bound.
A program may use at most 192 MiB of HBM per device.

v0:
```python
import math
import jax
import jax.numpy as jnp
from jax import lax
from jax.sharding import PartitionSpec as P

HEADS = 40
KV_HEADS = 8
HEAD_DIM = 128
NORM_EPS = 1e-06
ROPE_BASE = 1000000.0
MASKED = -1e30


def joined_2(part, axis, combine):
    gathered = jax.tree.map(lambda a: lax.all_gather(a, axis), part)

    def take(source):
        return jax.tree.map(lambda a: lax.dynamic_index_in_dim(a, source, 0, False), gathered)

    return lax.fori_loop(
        1, lax.axis_size(axis), lambda source, state: combine(state, take(source)), take(0)
    )


def rms_normalize(rows, gain):
    mean_square = jnp.mean(rows * rows, axis=-1, keepdims=True)
    return (rows * lax.rsqrt(mean_square + NORM_EPS) * gain.astype(jnp.float32)).astype(
        jnp.bfloat16
    )


def rotate(vectors, positions):
    half_dim = vectors.shape[-1] // 2
    frequency = ROPE_BASE ** (-2.0 * jnp.arange(half_dim, dtype=jnp.float32) / vectors.shape[-1])
    angles = positions.astype(jnp.float32)[..., None, None] * frequency
    cosine = jnp.cos(angles)
    sine_part = jnp.sin(angles)
    widened = vectors.astype(jnp.float32)
    first_half = widened[..., :half_dim]
    second = widened[..., half_dim:]
    joined = jnp.concatenate(
        [first_half * cosine - second * sine_part, second * cosine + first_half * sine_part],
        axis=-1,
    )
    return joined.astype(jnp.bfloat16)


def combine_partials(earlier, latter):
    top_one, total_one, sum_one = earlier
    top_two, total_two, sum_two = latter
    joined_top = jnp.maximum(top_one, top_two)
    scale_one = jnp.exp(top_one - joined_top)
    scale_two = jnp.exp(top_two - joined_top)
    return (
        joined_top,
        total_one * scale_one + total_two * scale_two,
        sum_one * scale_one[..., None] + sum_two * scale_two[..., None],
    )


def body(
    token_ids,
    lengths,
    embed_table,
    attn_gain,
    w_qkv,
    qkv_bias,
    cache_keys,
    cache_values,
    w_out,
    mlp_gain,
    w_gate,
    w_up,
    w_down,
):
    rank = lax.axis_index("seq")
    step_count, batch_count = token_ids.shape
    model_width = embed_table.shape[1]
    vocab_rows = embed_table.shape[0]
    query_width = HEADS * HEAD_DIM
    key_width = KV_HEADS * HEAD_DIM
    group_size = HEADS // KV_HEADS
    local_ids = token_ids - rank * vocab_rows
    inside = (local_ids >= 0) & (local_ids < vocab_rows)
    picked = jnp.take(embed_table, jnp.clip(local_ids, 0, vocab_rows - 1), axis=0)
    partial_rows = jnp.where(inside[..., None], picked.astype(jnp.float32), 0.0)
    stream = lax.psum(partial_rows, "seq")
    normed = rms_normalize(stream, attn_gain).reshape(-1, model_width)
    feature_rows = w_qkv.shape[0]
    normed_local = lax.dynamic_slice_in_dim(normed, rank * feature_rows, feature_rows, 1)
    joint_partial = jnp.dot(normed_local, w_qkv, preferred_element_type=jnp.float32)
    joint_summed = lax.psum(joint_partial, "seq")
    joint = (joint_summed + qkv_bias).astype(jnp.bfloat16).reshape(step_count, batch_count, -1)
    query_part = joint[..., :query_width].reshape(step_count, batch_count, HEADS, HEAD_DIM)
    key_part = joint[..., query_width : query_width + key_width].reshape(
        step_count, batch_count, KV_HEADS, HEAD_DIM
    )
    value_part = joint[..., query_width + key_width :].reshape(
        step_count, batch_count, KV_HEADS, HEAD_DIM
    )
    positions = lengths[None, :] + jnp.arange(step_count, dtype=jnp.int32)[:, None]
    queries = rotate(query_part, positions)
    new_keys = rotate(key_part, positions)
    grouped = queries.reshape(step_count, batch_count, KV_HEADS, group_size, HEAD_DIM)
    score_scale = 1.0 / math.sqrt(HEAD_DIM)
    local_len = cache_keys.shape[1]
    key_blocks = cache_keys.reshape(batch_count, local_len, KV_HEADS, HEAD_DIM)
    value_blocks = cache_values.reshape(batch_count, local_len, KV_HEADS, HEAD_DIM)
    scores = (
        jnp.einsum("sbkgd,bpkd->bkgsp", grouped, key_blocks, preferred_element_type=jnp.float32)
        * score_scale
    )
    places = rank * local_len + jnp.arange(local_len, dtype=jnp.int32)
    valid = (places[None, :] < lengths[:, None])[:, None, None, None, :]
    masked = jnp.where(valid, scores, MASKED)
    local_top = jnp.max(masked, axis=-1)
    weights = jnp.where(valid, jnp.exp(masked - local_top[..., None]), 0.0)
    local_total = jnp.sum(weights, axis=-1)
    local_sum = jnp.einsum(
        "bkgsp,bpkd->bkgsd",
        weights.astype(jnp.bfloat16),
        value_blocks,
        preferred_element_type=jnp.float32,
    )
    merged_top, merged_total, merged_sum = joined_2(
        (local_top, local_total, local_sum), "seq", combine_partials
    )
    new_scores = (
        jnp.einsum("sbkgd,tbkd->bkgst", grouped, new_keys, preferred_element_type=jnp.float32)
        * score_scale
    )
    step_index = jnp.arange(step_count, dtype=jnp.int32)
    causal = step_index[:, None] >= step_index[None, :]
    new_masked = jnp.where(causal, new_scores, MASKED)
    final_top = jnp.maximum(merged_top, jnp.max(new_masked, axis=-1))
    rescale = jnp.exp(merged_top - final_top)
    new_weights = jnp.where(causal, jnp.exp(new_masked - final_top[..., None]), 0.0)
    final_total = merged_total * rescale + jnp.sum(new_weights, axis=-1)
    final_sum = merged_sum * rescale[..., None] + jnp.einsum(
        "bkgst,tbkd->bkgsd",
        new_weights.astype(jnp.bfloat16),
        value_part,
        preferred_element_type=jnp.float32,
    )
    attended = jnp.transpose(final_sum / final_total[..., None], (3, 0, 1, 2, 4))
    attended = attended.reshape(step_count, batch_count, query_width).astype(jnp.bfloat16)
    shard_cols = w_out.shape[1]
    projected = jnp.dot(
        attended.reshape(-1, query_width), w_out, preferred_element_type=jnp.float32
    )
    stream_shard = lax.dynamic_slice_in_dim(stream, rank * shard_cols, shard_cols, 2)
    mid_shard = stream_shard + projected.reshape(step_count, batch_count, shard_cols)
    squares = lax.psum(jnp.sum(mid_shard * mid_shard, axis=-1), "seq")
    row_scale = lax.rsqrt(squares / model_width + NORM_EPS)
    gain_shard = lax.dynamic_slice_in_dim(mlp_gain, rank * shard_cols, shard_cols, 0).astype(
        jnp.float32
    )
    normed_shard = (mid_shard * row_scale[..., None] * gain_shard).astype(jnp.bfloat16)
    normed_mid = lax.all_gather(normed_shard, "seq", axis=2, tiled=True)
    flat_rows = normed_mid.reshape(-1, model_width)
    gate = jnp.dot(flat_rows, w_gate, preferred_element_type=jnp.float32)
    upper = jnp.dot(flat_rows, w_up, preferred_element_type=jnp.float32)
    hidden = (jax.nn.silu(gate) * upper).astype(jnp.bfloat16)
    down_terms = jnp.dot(hidden, w_down, preferred_element_type=jnp.float32).reshape(
        step_count, batch_count, model_width
    )
    summed = lax.psum_scatter(down_terms, "seq", scatter_dimension=2, tiled=True)
    layer_out = (mid_shard + summed).astype(jnp.bfloat16)
    return (attended, layer_out)


def solution(mesh):
    return jax.shard_map(
        body,
        mesh=mesh,
        in_specs=(
            P(None, "parts"),
            P("parts"),
            P("seq", None),
            P(),
            P("seq", None),
            P(),
            P("parts", "seq", None),
            P("parts", "seq", None),
            P(None, "seq"),
            P(),
            P(None, "seq"),
            P(None, "seq"),
            P("seq", None),
        ),
        out_specs=(P(None, "parts", None), P(None, "parts", "seq")),
        check_vma=False,
    )
```

profile of v0, /device:TPU:0, one launch (start us, length us, event | category | flops | bytes accessed | tf_op | source)
XLA Modules:
  0.0 495.7 jit_solution(8823497209833906688)
XLA Ops:
  7.2 0.8 compare_and_fusion
  8.3 1.9 gather_fusion
  10.4 0.8 convert_select_fusion
  13.4 8.8 %copy.106 = bf16[512,8,8,128]{3,2,1,0:T(8,128)(2,1)} copy(bf16[512,8,8,128]{3,1,2,0:T(8,128)(2,1)} %bitcast.100) | data formatting | bytes 16777216
  22.2 7.1 %bitcast_bitcast_fusion.1 = bf16[2,2048,8,128,1]{3,2,1,0,4:T(8,128)(2,1)} fusion(bf16[2,2048,8,128]{3,2,1,0:T(8,128)(2,1)} %bitcast.97), kind=kLoop, calls=%fused_computation.12 | loop fusion | bytes 16777216 | tf_op jit(solution)/shard_map/reshape | solution.py:108
  29.3 8.8 %copy.107 = bf16[512,8,8,128]{3,2,1,0:T(8,128)(2,1)} copy(bf16[512,8,8,128]{3,1,2,0:T(8,128)(2,1)} %bitcast.101) | data formatting | bytes 16777216
  38.1 7.0 %bitcast_bitcast_fusion = bf16[2,2048,8,128,1]{3,2,1,0,4:T(8,128)(2,1)} fusion(bf16[2,2048,8,128]{3,2,1,0:T(8,128)(2,1)} %bitcast.98), kind=kLoop, calls=%fused_computation.11 | loop fusion | bytes 16777216 | tf_op jit(solution)/shard_map/reshape | solution.py:109
  45.2 57.9 %all-reduce.3.cloned.1.call-done = f32[4,2,5120]{2,1,0:T(2,128)} async-done(((f32[4,2,5120]{2,1,0:T(2,128)}), f32[4,2,5120]{2,1,0:T(2,128)}) %all-reduce.3.cloned.1.call-update) | async-done | bytes 163856 | tf_op jit(solution)/shard_map/psum | solution.py:88
  103.1 1.1 multiply_reduce_fusion
  104.2 1.1 multiply_convert_fusion
  105.3 3.7 fusion.47
  109.4 90.0 %all-reduce.5.cloned.1.call-done = f32[8,7168]{1,0:T(8,128)} async-done(((f32[8,7168]{1,0:T(8,128)}), f32[8,7168]{1,0:T(8,128)}) %all-reduce.5.cloned.1.call-update) | async-done | bytes 229392 | tf_op jit(solution)/shard_map/psum | solution.py:93
  199.4 1.0 add_convert_fusion
  201.2 6.3 %bitcast_reduce_fusion = (f32[2,8,5,4]{2,3,1,0:T(4,128)S(1)}, f32[2,8,4,5,2048]{4,3,2,1,0:T(8,128)S(1)}) fusion(pred[2,2048]{1,0:T(4,128)(4,1)S(1)} %broadcast_compare_fusion, bf16[2,2048,8,128,1]{3,2,1,0,4:T(8,128)(2,1)} %bitcast_bitcast_fusion.1, bf16[4,2,8,5,64]{4,3,0,2,1:T(8,128)(2,1)S(1)} %copy.69, bf16[4,2,8,5,64]{4,3,0,2,1:T(8,128)(2,1)S(1)} %copy.68), kind=kOutput, calls=%fused_computation.18 | convolution fusion | flops 169901760 | bytes 11097344 | tf_op jit(solution)/shard_map/sbkgd,bpkd->bkgsp/dot_general | solution.py:111
  207.6 3.1 fusion.4
  212.5 3.6 fusion.13
  216.2 23.1 %all-gather.1 = f32[32,8,5,4]{1,3,2,0:T(4,128)S(1)} all-gather(f32[2,8,5,4]{1,3,2,0:T(4,128)S(1)} %copy.72), channel_id=3, replica_groups=mesh['parts'=2,'seq'=16] {'seq'}, dimensions={0}, use_global_device_ids=true | all-gather | bytes 21760 | tf_op jit(solution)/shard_map/all_gather | solution.py:16
  240.1 19.3 %all-gather = f32[32,8,5,4]{1,3,2,0:T(4,128)S(1)} all-gather(f32[2,8,5,4]{1,3,2,0:T(4,128)S(1)} %copy.71), channel_id=2, replica_groups=mesh['parts'=2,'seq'=16] {'seq'}, dimensions={0}, use_global_device_ids=true | all-gather | bytes 21760 | tf_op jit(solution)/shard_map/all_gather | solution.py:16
  261.1 2.3 fusion.60
  263.4 0.9 slice.41
  265.1 57.2 %while.19 = (s32[]{:T(128)}, f32[2,8,5,4]{1,3,2,0:T(4,128)S(1)}, f32[2,8,5,4]{1,3,2,0:T(4,128)S(1)}, f32[2,8,5,4,128]{4,3,2,1,0:T(4,128)}, f32[16,2,8,5,4]{2,4,3...) while((s32[]{:T(128)}, f32[2,8,5,4]{1,3,2,0:T(4,128)S(1)}, ...), condition=%wide.region_6.7_spmd, body=%wide.region_5.6_spmd.sunk | while | flops 124805 | bytes 837271 | solution.py:21
  266.1 0.9 constant_dynamic-slice_fusion.2
  267.0 1.8 fusion.72
  269.9 0.9 constant_dynamic-slice_fusion.2
  270.9 1.8 fusion.72
  273.7 0.9 constant_dynamic-slice_fusion.2
  274.7 1.8 fusion.72
  277.6 0.9 constant_dynamic-slice_fusion.2
  278.5 1.8 fusion.72
  281.4 0.9 constant_dynamic-slice_fusion.2
  282.3 1.8 fusion.72
  285.2 0.9 constant_dynamic-slice_fusion.2
  286.1 1.8 fusion.72
  289.0 0.9 constant_dynamic-slice_fusion.2
  290.0 1.8 fusion.72
  292.8 0.9 constant_dynamic-slice_fusion.2
  293.8 1.8 fusion.72
  296.6 0.9 constant_dynamic-slice_fusion.2
  297.6 1.8 fusion.72
  300.5 0.9 constant_dynamic-slice_fusion.2
  301.4 1.8 fusion.72
  304.3 0.9 constant_dynamic-slice_fusion.2
  305.2 1.8 fusion.72
  308.1 0.9 constant_dynamic-slice_fusion.2
  309.0 1.8 fusion.72
  311.9 0.9 constant_dynamic-slice_fusion.2
  312.8 1.8 fusion.72
  315.7 0.9 constant_dynamic-slice_fusion.2
  316.6 1.8 fusion.72
  319.5 0.9 constant_dynamic-slice_fusion.2
  320.5 1.8 fusion.72
  322.5 1.1 fusion.31
  323.7 1.4 fusion.23
  325.1 1.8 multiply_reduce_fusion.1
  327.0 30.7 %psum.23 = f32[4,2]{1,0:T(4,128)S(1)} all-reduce(f32[4,2]{1,0:T(4,128)S(1)} %get-tuple-element.245), channel_id=1, replica_groups=mesh['parts'=2,'seq'=16] {'seq'}, use_global_device_ids=true, to_apply=%region_10.11 | all-reduce | flops 8 | bytes 64 | tf_op jit(solution)/shard_map/psum | solution.py:154
  357.9 33.2 %all_gather.27 = bf16[4,2,5120]{0,1,2:T(2,128)(2,1)} all-gather(bf16[4,2,320]{0,1,2:T(2,128)(2,1)S(1)} %copy.85), channel_id=1, replica_groups=mesh['parts'=2,'seq'=16] {'seq'}, dimensions={2}, use_global_device_ids=true | all-gather | bytes 87040 | tf_op jit(solution)/shard_map/all_gather | solution.py:160
  391.2 5.2 %copy.86 = bf16[4,2,5120]{2,1,0:T(2,128)(2,1)S(1)} copy(bf16[4,2,5120]{0,1,2:T(2,128)(2,1)} %all_gather.27) | data formatting | bytes 163840 | tf_op jit(solution)/shard_map/all_gather | solution.py:160
  396.5 5.4 %fusion.61 = f32[8,1024]{1,0:T(8,128)S(1)} fusion(bf16[8,5120]{1,0:T(8,128)(2,1)S(1)} %reshape.133, bf16[5120,1024]{1,0:T(8,128)(2,1)} %param.25), kind=kOutput, calls=%fused_computation.105 | convolution fusion | flops 83886080 | bytes 10600448 | tf_op jit(solution)/shard_map/dot_general | solution.py:162
  401.9 9.8 %fusion.30 = f32[8,5120]{1,0:T(8,128)S(1)} fusion(bf16[1024,5120]{1,0:T(8,128)(2,1)} %param.27, bf16[8,5120]{1,0:T(8,128)(2,1)S(1)} %reshape.133, bf16[5120,1024]{1,0:T(8,128)(2,1)} %param.26, f32[8,1024]{1,0:T(8,128)S(1)} %fusion.61), kind=kOutput, calls=%fused_computation.42 | convolution fusion | flops 167821312 | bytes 21250048 | tf_op jit(solution)/shard_map/dot_general | solution.py:165
  412.5 5.9 %copy.99 = f32[4,2,5120]{0,1,2:T(2,128)} copy(f32[4,2,5120]{2,1,0:T(2,128)} %reshape.134) | data formatting | bytes 327680
  418.4 6.0 %reshape.161 = f32[5120,8]{1,0:T(8,128)} reshape(f32[5120,2,4]{2,1,0:T(2,128)} %bitcast.99) | data formatting | bytes 327680
  424.4 61.2 %reduce-scatter.4.cloned.1.call-done = f32[320,8]{1,0:T(8,128)} async-done(((f32[5120,8]{1,0:T(8,128)}), f32[320,8]{1,0:T(8,128)}) %reduce-scatter.4.cloned.1.call-update) | async-done | bytes 10256
  485.5 1.9 reshape.162
  487.4 1.1 copy.88
  (125 shorter events, 26.8 us)
Async XLA Ops:
  7.2 317.9 %copy-start = (bf16[5120,320]{0,1:T(8,128)(2,1)S(1)}, bf16[5120,320]{0,1:T(8,128)(2,1)}, u32[]{:S(2)}) copy-start(bf16[5120,320]{0,1:T(8,128)(2,1)} %param.23) | copy-start | bytes 9830404
  7.2 95.9 %all-reduce.3.cloned.1.call-start = ((), (), s32[]{:S(2)}) async-start(), calls=%async_computation.1 | async-start | bytes 327680 | tf_op jit(solution)/shard_map/psum | solution.py:88
  11.2 188.2 %all-reduce.5.cloned.1.call-start = ((), (), s32[]{:S(2)}) async-start(), calls=%async_computation.2 | async-start | bytes 458752 | tf_op jit(solution)/shard_map/psum | solution.py:93
  45.2 154.3 %copy-start.9 = (f32[7168]{0:T(1024)S(1)}, f32[7168]{0:T(1024)}, u32[]{:S(2)}) copy-start(f32[7168]{0:T(1024)} %param.20) | copy-start | bytes 86020
  109.1 154.3 %all-gather.5.cloned.1.call-start = ((), (), s32[]{:S(2)}) async-start(), calls=%async_computation.3 | async-start | bytes 2785280 | tf_op jit(solution)/shard_map/all_gather | solution.py:16
  200.4 0.7 copy-start.5
  201.1 6.5 %slice-start = ((s8[8388608]{0:T(1024)(128)(4,1)}), s8[4194304]{0:T(1024)(128)(4,1)S(1)}, s32[]{:S(2)}) async-start(s8[8388608]{0:T(1024)(128)(4,1)} %bitcast.102), calls=%async_computation.5 | async-start | bytes 8388608
  201.2 6.4 %copy-start.4 = (bf16[4,2,8,5,64]{4,3,0,2,1:T(8,128)(2,1)}, bf16[4,2,8,5,64]{4,3,0,2,1:T(8,128)(2,1)S(1)}, u32[]{:S(2)}) copy-start(bf16[4,2,8,5,64]{4,3,0,2,1:T(8,128)(2,1)S(1)} %copy.69) | copy-start | bytes 122884
  201.2 6.4 %slice-start.1 = ((s8[8388608]{0:T(1024)(128)(4,1)}), s8[4194304]{0:T(1024)(128)(4,1)S(1)}, s32[]{:S(2)}) async-start(s8[8388608]{0:T(1024)(128)(4,1)} %bitcast.102), calls=%async_computation.6 | async-start | bytes 8388608
  207.5 3.2 copy-start.1
  211.5 274.0 %reduce-scatter.4.cloned.1.call-start = ((), (), s32[]{:S(2)}) async-start(), calls=%async_computation.4 | async-start | bytes 2785280
  239.3 0.7 copy-start.2
  259.4 0.7 copy-start.3
  325.1 32.6 %copy-start.6 = (bf16[4,2,5120]{2,1,0:T(2,128)(2,1)}, bf16[4,2,5120]{2,1,0:T(2,128)(2,1)S(1)}, u32[]{:S(2)}) copy-start(bf16[4,2,5120]{2,1,0:T(2,128)(2,1)S(1)} %convert_element_type.77) | copy-start | bytes 245764
  327.0 30.7 %copy-start.7 = (f32[4,2,320]{2,1,0:T(2,128)}, f32[4,2,320]{2,1,0:T(2,128)S(1)}, u32[]{:S(2)}) copy-start(f32[4,2,320]{2,1,0:T(2,128)S(1)} %get-tuple-element.246) | copy-start | bytes 30724
  418.4 70.1 %copy-start.8 = (f32[4,2,320]{2,1,0:T(2,128)S(1)}, f32[4,2,320]{2,1,0:T(2,128)}, u32[]{:S(2)}) copy-start(f32[4,2,320]{2,1,0:T(2,128)} %copy-done.7) | copy-start | bytes 30724
Sparse Core Ops, SparseCore 0:
  11.4 91.6 all-reduce.2
  109.2 90.1 all-reduce.4
  211.6 46.0 all-gather.4
  424.5 61.0 reduce-scatter.3
where the time goes:
time: 499 us; the launch traced here: 496 us
  waiting for transfers between devices  209 us (42%)
  blocking collectives  106 us (21%)
  local copies, waits for them, and re-layouts  78.3 us (16%)
  other arithmetic  53.3 us (11%)
  matrix products  34 us (7%)
  between operations  14.1 us (3%)
    psum x1, waiting for transfers between devices, body(): joint_summed = lax.psum(joint_partial, 'seq')  90 us
    unnamed x5, waiting for transfers between devices  61.2 us
    psum x1, waiting for transfers between devices, body(): stream = lax.psum(partial_rows, 'seq')  57.9 us
    all_gather x2, blocking collectives, joined_2(): gathered = jax.tree.map(lambda a: lax.all_gather(a, axis), part)  42.5 us
    all_gather x1, blocking collectives, body(): normed_mid = lax.all_gather(normed_shard, 'seq', axis=2, tiled=True)  33.2 us
    unnamed x29, local copies, waits for them, and re-layouts  33.1 us
    psum x1, blocking collectives, body(): squares = lax.psum(jnp.sum(mid_shard * mid_shard, axis=-1), 'seq')  30.7 us
    add x15, other arithmetic, combine_partials(): sum_one * scale_one[..., None] + sum_two * scale_two[..., None]  27.3 us
  transfers between devices with their start and end apart: 4, of which 3 were waited for; matrix products, arithmetic and copies ran while one was open for 8% of the time, Pallas kernels for 0%

commit v1 on v0

--- a/solution.py
+++ b/solution.py
@@ -157,7 +157,8 @@
         jnp.float32
     )
     normed_shard = (mid_shard * row_scale[..., None] * gain_shard).astype(jnp.bfloat16)
-    normed_mid = lax.all_gather(normed_shard, "seq", axis=2, tiled=True)
+    state_next = lax.all_gather(normed_shard, axis_name="seq")
+    normed_mid = jnp.concatenate(state_next, 2)
     flat_rows = normed_mid.reshape(-1, model_width)
     gate = jnp.dot(flat_rows, w_gate, preferred_element_type=jnp.float32)
     upper = jnp.dot(flat_rows, w_up, preferred_element_type=jnp.float32)

time: 499 us -> 479 us (0.960)
  blocking collectives: 106 us -> 90.7 us
  local copies, waits for them, and re-layouts: 78.3 us -> 73 us
    all_gather x1, blocking collectives: 33.2 us -> 17.6 us  [body(): state_next = lax.all_gather(normed_shard, axis_name='seq')]
    all_gather x1, local copies, waits for them, and re-layouts: 5.21 us -> 0.01 us  [body(): state_next = lax.all_gather(normed_shard, axis_name='seq')]
  transfers between devices with their start and end apart: 4 -> 4, of which waited for: 3 -> 3; matrix products, arithmetic and copies ran while one was open for 8% -> 9% of each run, Pallas kernels for 0% -> 0%
where the time goes in v1:
time: 479 us; the launch traced here: 476 us
  waiting for transfers between devices  211 us (44%)
  blocking collectives  90.7 us (19%)
  local copies, waits for them, and re-layouts  73 us (15%)
  other arithmetic  53.3 us (11%)
  matrix products  34 us (7%)
  between operations  14.1 us (3%)
    psum x1, waiting for transfers between devices, body(): joint_summed = lax.psum(joint_partial, 'seq')  90 us
    unnamed x5, waiting for transfers between devices  62.6 us
    psum x1, waiting for transfers between devices, body(): stream = lax.psum(partial_rows, 'seq')  57.9 us
    all_gather x2, blocking collectives, joined_2(): gathered = jax.tree.map(lambda a: lax.all_gather(a, axis), part)  42.5 us
    unnamed x29, local copies, waits for them, and re-layouts  33.1 us
    psum x1, blocking collectives, body(): squares = lax.psum(jnp.sum(mid_shard * mid_shard, axis=-1), 'seq')  30.7 us
    add x15, other arithmetic, combine_partials(): sum_one * scale_one[..., None] + sum_two * scale_two[..., None]  27.3 us
    all_gather x1, blocking collectives, body(): state_next = lax.all_gather(normed_shard, axis_name='seq')  17.6 us
  transfers between devices with their start and end apart: 4, of which 3 were waited for; matrix products, arithmetic and copies ran while one was open for 9% of the time, Pallas kernels for 0%

profile of v1, /device:TPU:0, one launch (start us, length us, event | category | flops | bytes accessed | tf_op | source)
XLA Modules:
  0.0 476.1 jit_solution(7484312634553994906)
XLA Ops:
  7.2 0.8 compare_and_fusion
  8.3 1.9 gather_fusion
  10.4 0.8 convert_select_fusion
  13.4 8.8 %copy.105 = bf16[512,8,8,128]{3,2,1,0:T(8,128)(2,1)} copy(bf16[512,8,8,128]{3,1,2,0:T(8,128)(2,1)} %bitcast.106) | data formatting | bytes 16777216
  22.2 7.1 %bitcast_bitcast_fusion.1 = bf16[2,2048,8,128,1]{3,2,1,0,4:T(8,128)(2,1)} fusion(bf16[2,2048,8,128]{3,2,1,0:T(8,128)(2,1)} %bitcast.103), kind=kLoop, calls=%fused_computation.12 | loop fusion | bytes 16777216 | tf_op jit(solution)/shard_map/reshape | solution.py:108
  29.3 8.8 %copy.106 = bf16[512,8,8,128]{3,2,1,0:T(8,128)(2,1)} copy(bf16[512,8,8,128]{3,1,2,0:T(8,128)(2,1)} %bitcast.107) | data formatting | bytes 16777216
  38.1 7.0 %bitcast_bitcast_fusion = bf16[2,2048,8,128,1]{3,2,1,0,4:T(8,128)(2,1)} fusion(bf16[2,2048,8,128]{3,2,1,0:T(8,128)(2,1)} %bitcast.104), kind=kLoop, calls=%fused_computation.11 | loop fusion | bytes 16777216 | tf_op jit(solution)/shard_map/reshape | solution.py:109
  45.2 57.9 %all-reduce.3.cloned.1.call-done = f32[4,2,5120]{2,1,0:T(2,128)} async-done(((f32[4,2,5120]{2,1,0:T(2,128)}), f32[4,2,5120]{2,1,0:T(2,128)}) %all-reduce.3.cloned.1.call-update) | async-done | bytes 163856 | tf_op jit(solution)/shard_map/psum | solution.py:88
  103.1 1.1 multiply_reduce_fusion
  104.2 1.1 multiply_convert_fusion
  105.3 3.7 fusion.47
  109.4 90.0 %all-reduce.5.cloned.1.call-done = f32[8,7168]{1,0:T(8,128)} async-done(((f32[8,7168]{1,0:T(8,128)}), f32[8,7168]{1,0:T(8,128)}) %all-reduce.5.cloned.1.call-update) | async-done | bytes 229392 | tf_op jit(solution)/shard_map/psum | solution.py:93
  199.4 1.0 add_convert_fusion
  201.2 6.3 %bitcast_reduce_fusion = (f32[2,8,5,4]{2,3,1,0:T(4,128)S(1)}, f32[2,8,4,5,2048]{4,3,2,1,0:T(8,128)S(1)}) fusion(pred[2,2048]{1,0:T(4,128)(4,1)S(1)} %broadcast_compare_fusion, bf16[2,2048,8,128,1]{3,2,1,0,4:T(8,128)(2,1)} %bitcast_bitcast_fusion.1, bf16[4,2,8,5,64]{4,3,0,2,1:T(8,128)(2,1)S(1)} %copy.69, bf16[4,2,8,5,64]{4,3,0,2,1:T(8,128)(2,1)S(1)} %copy.68), kind=kOutput, calls=%fused_computation.18 | convolution fusion | flops 169901760 | bytes 11097344 | tf_op jit(solution)/shard_map/sbkgd,bpkd->bkgsp/dot_general | solution.py:111
  207.6 3.1 fusion.4
  212.5 3.6 fusion.13
  216.2 23.1 %all-gather.1 = f32[32,8,5,4]{1,3,2,0:T(4,128)S(1)} all-gather(f32[2,8,5,4]{1,3,2,0:T(4,128)S(1)} %copy.72), channel_id=3, replica_groups=mesh['parts'=2,'seq'=16] {'seq'}, dimensions={0}, use_global_device_ids=true | all-gather | bytes 21760 | tf_op jit(solution)/shard_map/all_gather | solution.py:16
  240.1 19.3 %all-gather = f32[32,8,5,4]{1,3,2,0:T(4,128)S(1)} all-gather(f32[2,8,5,4]{1,3,2,0:T(4,128)S(1)} %copy.71), channel_id=2, replica_groups=mesh['parts'=2,'seq'=16] {'seq'}, dimensions={0}, use_global_device_ids=true | all-gather | bytes 21760 | tf_op jit(solution)/shard_map/all_gather | solution.py:16
  261.1 2.3 fusion.60
  263.4 0.9 slice.41
  265.1 57.2 %while.19 = (s32[]{:T(128)}, f32[2,8,5,4]{1,3,2,0:T(4,128)S(1)}, f32[2,8,5,4]{1,3,2,0:T(4,128)S(1)}, f32[2,8,5,4,128]{4,3,2,1,0:T(4,128)}, f32[16,2,8,5,4]{2,4,3...) while((s32[]{:T(128)}, f32[2,8,5,4]{1,3,2,0:T(4,128)S(1)}, ...), condition=%wide.region_6.7_spmd, body=%wide.region_5.6_spmd.sunk | while | flops 124805 | bytes 837271 | solution.py:21
  266.1 0.9 constant_dynamic-slice_fusion.2
  267.0 1.8 fusion.72
  269.9 0.9 constant_dynamic-slice_fusion.2
  270.9 1.8 fusion.72
  273.7 0.9 constant_dynamic-slice_fusion.2
  274.7 1.8 fusion.72
  277.6 0.9 constant_dynamic-slice_fusion.2
  278.5 1.8 fusion.72
  280.3 0.8 fusion.71
  281.4 0.9 constant_dynamic-slice_fusion.2
  282.3 1.8 fusion.72
  285.2 0.9 constant_dynamic-slice_fusion.2
  286.1 1.8 fusion.72
  289.0 0.9 constant_dynamic-slice_fusion.2
  290.0 1.8 fusion.72
  292.8 0.9 constant_dynamic-slice_fusion.2
  293.8 1.8 fusion.72
  296.6 0.9 constant_dynamic-slice_fusion.2
  297.6 1.8 fusion.72
  300.5 0.9 constant_dynamic-slice_fusion.2
  301.4 1.8 fusion.72
  304.3 0.9 constant_dynamic-slice_fusion.2
  305.2 1.8 fusion.72
  308.1 0.9 constant_dynamic-slice_fusion.2
  309.0 1.8 fusion.72
  311.9 0.9 constant_dynamic-slice_fusion.2
  312.8 1.8 fusion.72
  315.7 0.9 constant_dynamic-slice_fusion.2
  316.6 1.8 fusion.72
  319.5 0.9 constant_dynamic-slice_fusion.2
  320.5 1.8 fusion.72
  322.5 1.1 fusion.31
  323.7 1.4 fusion.23
  325.1 1.8 multiply_reduce_fusion.1
  327.0 30.7 %psum.23 = f32[4,2]{1,0:T(4,128)S(1)} all-reduce(f32[4,2]{1,0:T(4,128)S(1)} %get-tuple-element.245), channel_id=1, replica_groups=mesh['parts'=2,'seq'=16] {'seq'}, use_global_device_ids=true, to_apply=%region_10.11 | all-reduce | flops 8 | bytes 64 | tf_op jit(solution)/shard_map/psum | solution.py:154
  357.8 17.6 %all-gather.3 = bf16[64,2,320]{2,1,0:T(2,128)(2,1)S(1)} all-gather(bf16[4,2,320]{2,1,0:T(2,128)(2,1)S(1)} %multiply_convert_fusion.1), channel_id=5, replica_groups=mesh['parts'=2,'seq'=16] {'seq'}, dimensions={0}, use_global_device_ids=true | all-gather | bytes 87040 | tf_op jit(solution)/shard_map/all_gather | solution.py:160
  375.5 5.4 %fusion.61 = f32[8,1024]{1,0:T(8,128)S(1)} fusion(bf16[8,5120]{1,0:T(8,128)(2,1)S(1)} %reshape_reshape.3, bf16[5120,1024]{1,0:T(8,128)(2,1)} %param.25), kind=kOutput, calls=%fused_computation.106 | convolution fusion | flops 83886080 | bytes 10600448 | tf_op jit(solution)/shard_map/dot_general | solution.py:163
  380.9 9.8 %fusion.30 = f32[8,5120]{1,0:T(8,128)S(1)} fusion(bf16[1024,5120]{1,0:T(8,128)(2,1)} %param.27, bf16[8,5120]{1,0:T(8,128)(2,1)S(1)} %reshape_reshape.3, bf16[5120,1024]{1,0:T(8,128)(2,1)} %param.26, f32[8,1024]{1,0:T(8,128)S(1)} %fusion.61), kind=kOutput, calls=%fused_computation.42 | convolution fusion | flops 167821312 | bytes 21250048 | tf_op jit(solution)/shard_map/dot_general | solution.py:166
  391.5 5.9 %copy.98 = f32[4,2,5120]{0,1,2:T(2,128)} copy(f32[4,2,5120]{2,1,0:T(2,128)} %reshape.134) | data formatting | bytes 327680
  397.4 6.0 %reshape.162 = f32[5120,8]{1,0:T(8,128)} reshape(f32[5120,2,4]{2,1,0:T(2,128)} %bitcast.105) | data formatting | bytes 327680
  403.4 62.6 %reduce-scatter.4.cloned.1.call-done = f32[320,8]{1,0:T(8,128)} async-done(((f32[5120,8]{1,0:T(8,128)}), f32[320,8]{1,0:T(8,128)}) %reduce-scatter.4.cloned.1.call-update) | async-done | bytes 10256
  466.0 1.9 reshape.163
  467.9 1.1 copy.87
  (124 shorter events, 25.9 us)
Async XLA Ops:
  7.2 317.9 %copy-start = (bf16[5120,320]{0,1:T(8,128)(2,1)S(1)}, bf16[5120,320]{0,1:T(8,128)(2,1)}, u32[]{:S(2)}) copy-start(bf16[5120,320]{0,1:T(8,128)(2,1)} %param.23) | copy-start | bytes 9830404
  7.2 95.9 %all-reduce.3.cloned.1.call-start = ((), (), s32[]{:S(2)}) async-start(), calls=%async_computation.1 | async-start | bytes 327680 | tf_op jit(solution)/shard_map/psum | solution.py:88
  11.2 188.2 %all-reduce.5.cloned.1.call-start = ((), (), s32[]{:S(2)}) async-start(), calls=%async_computation.2 | async-start | bytes 458752 | tf_op jit(solution)/shard_map/psum | solution.py:93
  45.2 154.3 %copy-start.9 = (f32[7168]{0:T(1024)S(1)}, f32[7168]{0:T(1024)}, u32[]{:S(2)}) copy-start(f32[7168]{0:T(1024)} %param.20) | copy-start | bytes 86020
  109.1 154.3 %all-gather.6.cloned.1.call-start = ((), (), s32[]{:S(2)}) async-start(), calls=%async_computation.3 | async-start | bytes 2785280 | tf_op jit(solution)/shard_map/all_gather | solution.py:16
  200.4 0.7 copy-start.5
  201.1 6.5 %slice-start = ((s8[8388608]{0:T(1024)(128)(4,1)}), s8[4194304]{0:T(1024)(128)(4,1)S(1)}, s32[]{:S(2)}) async-start(s8[8388608]{0:T(1024)(128)(4,1)} %bitcast.108), calls=%async_computation.5 | async-start | bytes 8388608
  201.2 6.4 %copy-start.4 = (bf16[4,2,8,5,64]{4,3,0,2,1:T(8,128)(2,1)}, bf16[4,2,8,5,64]{4,3,0,2,1:T(8,128)(2,1)S(1)}, u32[]{:S(2)}) copy-start(bf16[4,2,8,5,64]{4,3,0,2,1:T(8,128)(2,1)S(1)} %copy.69) | copy-start | bytes 122884
  201.2 6.4 %slice-start.1 = ((s8[8388608]{0:T(1024)(128)(4,1)}), s8[4194304]{0:T(1024)(128)(4,1)S(1)}, s32[]{:S(2)}) async-start(s8[8388608]{0:T(1024)(128)(4,1)} %bitcast.108), calls=%async_computation.6 | async-start | bytes 8388608
  207.5 3.2 copy-start.1
  211.5 254.5 %reduce-scatter.4.cloned.1.call-start = ((), (), s32[]{:S(2)}) async-start(), calls=%async_computation.4 | async-start | bytes 2785280
  239.3 0.7 copy-start.2
  259.4 0.7 copy-start.3
  325.1 50.2 %copy-start.6 = (bf16[4,2,5120]{2,1,0:T(2,128)(2,1)}, bf16[4,2,5120]{2,1,0:T(2,128)(2,1)S(1)}, u32[]{:S(2)}) copy-start(bf16[4,2,5120]{2,1,0:T(2,128)(2,1)S(1)} %convert_element_type.77) | copy-start | bytes 245764
  327.0 48.4 %copy-start.7 = (f32[4,2,320]{2,1,0:T(2,128)}, f32[4,2,320]{2,1,0:T(2,128)S(1)}, u32[]{:S(2)}) copy-start(f32[4,2,320]{2,1,0:T(2,128)S(1)} %get-tuple-element.246) | copy-start | bytes 30724
  397.4 71.5 %copy-start.8 = (f32[4,2,320]{2,1,0:T(2,128)S(1)}, f32[4,2,320]{2,1,0:T(2,128)}, u32[]{:S(2)}) copy-start(f32[4,2,320]{2,1,0:T(2,128)} %copy-done.7) | copy-start | bytes 30724
Sparse Core Ops, SparseCore 0:
  11.4 91.6 all-reduce.2
  109.2 90.1 all-reduce.4
  211.6 46.0 all-gather.5
  403.5 62.4 reduce-scatter.3
